TPU v7x, 32 devices: a whole 2x2x4 slice. The times are simulated.
32 devices in a mesh: rep: 8 (over z, core), tp: 4 (over y, x).
Axes of the slice: x: 2, y: 2, z: 4, core: 2. Of those that a mesh axis runs over, the one named last changes fastest.
Arguments:
- delta_query: bfloat16 [8, 2, 2048, 3072], P('rep', None, None, 'tp'), may hold values from -6 to 6
- master_query: float32 [2, 2048, 3072], P(None, 'rep', 'tp'), may hold values from -3 to 3
- moment_query: float32 [2, 2048, 3072], P(None, 'rep', 'tp'), may hold values from -3 to 3
- delta_latent: bfloat16 [8, 2, 512, 4096], P('rep', None, None, 'tp'), may hold values from -6 to 6
- master_latent: float32 [2, 512, 4096], P(None, 'rep', 'tp'), may hold values from -3 to 3
- moment_latent: float32 [2, 512, 4096], P(None, 'rep', 'tp'), may hold values from -3 to 3
- delta_output: bfloat16 [8, 2, 2048, 2048], P('rep', None, 'tp'), may hold values from -6 to 6
- master_output: float32 [2, 2048, 2048], P(None, 'tp', 'rep'), may hold values from -3 to 3
- moment_output: float32 [2, 2048, 2048], P(None, 'tp', 'rep'), may hold values from -3 to 3
Outputs:
- params_query: bfloat16 [2, 2048, 3072], P(None, None, 'tp')
- new_master_query: float32 [2, 2048, 3072], P(None, 'rep', 'tp')
- new_moment_query: float32 [2, 2048, 3072], P(None, 'rep', 'tp')
- params_latent: bfloat16 [2, 512, 4096], P(None, None, 'tp')
- new_master_latent: float32 [2, 512, 4096], P(None, 'rep', 'tp')
- new_moment_latent: float32 [2, 512, 4096], P(None, 'rep', 'tp')
- params_output: bfloat16 [2, 2048, 2048], P(None, 'tp')
- new_master_output: float32 [2, 2048, 2048], P(None, 'tp', 'rep')
- new_moment_output: float32 [2, 2048, 2048], P(None, 'tp', 'rep')
All inputs are finite; a program needn't handle non-finite values.
Results may differ from a plain program's by a relative error of at most 0.012.
Values may be sent and summed in bfloat16 or wider, within the bound.
A program may use at most 128 MiB of HBM per device.

v0:
```python
import functools

import jax
import jax.numpy as jnp
from jax import lax
from jax.experimental import pallas as pl
from jax.experimental.pallas import tpu as pltpu
from jax.sharding import PartitionSpec as P

OUTER_RATE = 0.7
OUTER_MOMENTUM = 0.9
MESH = pl.DeviceIdType.MESH
PIECES = 16
LEAD = 3


def plan(shapes, pieces):
    cuts = []
    for layers, rows, cols in shapes:
        if pieces % layers:
            return None
        per_layer = pieces // layers
        by_row = per_layer
        while by_row > 1 and (rows % by_row or (rows // by_row) % 16):
            by_row //= 2
        by_col = per_layer // by_row
        if by_row * by_col != per_layer or cols % by_col or (cols // by_col) % 128:
            return None
        cuts.append((per_layer, by_col, rows // by_row, cols // by_col))
    return cuts


def kernel(n, cuts, width, own_shapes, *refs):
    deltas, masters, moments = refs[0:9:3], refs[1:9:3], refs[2:9:3]
    params, new_masters, new_moments = refs[9:18:3], refs[10:18:3], refs[11:18:3]
    (theirs, mine, up_in, down_in, gathered, master, moment) = refs[18:25]
    (theirs_sem, mine_sem, up_sem, down_sem, gather_sem, state_sem,
     gather_up_sem, gather_down_sem, total_sem) = refs[25:]
    m = n // 2
    pieces = theirs.shape[0]
    me = lax.axis_index("rep")
    z, core = me // 2, me % 2
    partner = z * 2 + 1 - core
    above, below = (z + 1) * 2 + core, (z - 1) * 2 + core
    first, last = z == 0, z == m - 1

    def blocks(k):
        found, at = [], 0
        for a, (per_layer, by_col, rows, cols) in enumerate(cuts):
            layer, part = k // per_layer, k % per_layer
            row, col = (part // by_col) * rows, (part % by_col) * cols
            for b in range(cols // width):
                found.append((a, layer, row, rows, col + b * width, at))
                at += rows
        return found

    def whole_slice(a, layer, row, rows, col, owner):
        own_rows, own_cols = own_shapes[a][1:]
        if a < 2:
            row = row + owner * own_rows
        else:
            col = col + owner * own_cols
        return (layer, pl.ds(pl.multiple_of(row, 16), rows), pl.ds(pl.multiple_of(col, 128), width))

    def own_slice(a, layer, row, rows, col):
        return (layer, pl.ds(pl.multiple_of(row, 16), rows), pl.ds(pl.multiple_of(col, 128), width))

    def remote(src, dst, send, recv, rank):
        return pltpu.make_async_remote_copy(
            src_ref=src, dst_ref=dst, send_sem=send, recv_sem=recv,
            device_id={"rep": rank}, device_id_type=MESH,
        )

    def wait_bytes(ref, sem):
        pltpu.make_async_copy(ref, ref, sem).wait()

    def fetch(k):
        for i in range(m):
            j = jnp.where(first, m - 1 - i, i)
            for a, layer, row, rows, col, at in blocks(k):
                there = pl.ds(at, rows)
                remote(
                    deltas[a].at[(0,) + whole_slice(a, layer, row, rows, col, 2 * j + 1 - core)],
                    theirs.at[k, j, there], total_sem.at[0], theirs_sem.at[k, j], partner,
                ).start()
                pltpu.make_async_copy(
                    deltas[a].at[(0,) + whole_slice(a, layer, row, rows, col, 2 * j + core)],
                    mine.at[k, j, there], mine_sem.at[k, j],
                ).start()
        for a, layer, row, rows, col, at in blocks(k):
            there, own = pl.ds(at, rows), own_slice(a, layer, row, rows, col)
            pltpu.make_async_copy(masters[a].at[own], master.at[k, there], state_sem.at[k]).start()
            pltpu.make_async_copy(moments[a].at[own], moment.at[k, there], state_sem.at[k]).start()

    def pair_sum(k, j):
        wait_bytes(theirs.at[k, j], theirs_sem.at[k, j])
        wait_bytes(mine.at[k, j], mine_sem.at[k, j])
        return theirs[k, j].astype(jnp.float32) + mine[k, j].astype(jnp.float32)

    def send_up(k, j):
        remote(mine.at[k, j], up_in.at[k, j], total_sem.at[1], up_sem.at[k, j], above).start()

    def send_down(k, j):
        remote(mine.at[k, j], down_in.at[k, j], total_sem.at[1], down_sem.at[k, j], below).start()

    def begin(k):
        @pl.when(first | last)
        def _():
            for i in range(m - 1):
                j = jnp.where(first, m - 1 - i, i)
                mine[k, j] = pair_sum(k, j).astype(jnp.bfloat16)

                @pl.when(first)
                def _():
                    send_up(k, j)

                @pl.when(last)
                def _():
                    send_down(k, j)

    def forward(s, k):
        up_j = m - 1 + z - s

        @pl.when((z >= 1) & (z <= s) & (z < m - 1))
        def _():
            running = pair_sum(k, up_j)
            wait_bytes(up_in.at[k, up_j], up_sem.at[k, up_j])
            mine[k, up_j] = (running + up_in[k, up_j].astype(jnp.float32)).astype(jnp.bfloat16)
            send_up(k, up_j)

        down_j = s - (m - 1 - z)

        @pl.when((z < m - 1) & (m - 1 - z <= s) & (z >= 1))
        def _():
            running = pair_sum(k, down_j)
            wait_bytes(down_in.at[k, down_j], down_sem.at[k, down_j])
            mine[k, down_j] = (running + down_in[k, down_j].astype(jnp.float32)).astype(jnp.bfloat16)
            send_down(k, down_j)

    def hand_on(k, j, up, down):
        chunk = gathered.at[k, j]

        @pl.when(up)
        def _():
            remote(chunk, chunk, gather_up_sem.at[k, j], gather_sem.at[k, j], above).start()

        @pl.when(down)
        def _():
            remote(chunk, chunk, gather_down_sem.at[k, j], gather_sem.at[k, j], below).start()

        for a, layer, row, rows, col, at in blocks(k):
            source = gathered.at[k, j, pl.ds(at, rows)]
            target = params[a].at[whole_slice(a, layer, row, rows, col, 2 * j + core)]
            remote(source, target, total_sem.at[2], total_sem.at[3], partner).start()
            pltpu.make_async_copy(source, target, total_sem.at[4]).start()

    def update(k):
        total = pair_sum(k, z)
        pltpu.make_async_copy(master.at[k], master.at[k], state_sem.at[k]).wait()
        pltpu.make_async_copy(moment.at[k], moment.at[k], state_sem.at[k]).wait()
        mine_total = total

        def finish(summed):
            average = summed / n
            momentum = OUTER_MOMENTUM * moment[k] + average
            updated = master[k] - OUTER_RATE * (average + OUTER_MOMENTUM * momentum)
            moment[k] = momentum
            master[k] = updated
            gathered[k, z] = updated.astype(jnp.bfloat16)

        @pl.when(z > 0)
        def _():
            wait_bytes(up_in.at[k, z], up_sem.at[k, z])

        @pl.when(z < m - 1)
        def _():
            wait_bytes(down_in.at[k, z], down_sem.at[k, z])

        @pl.when(first)
        def _():
            finish(mine_total + down_in[k, z].astype(jnp.float32))

        @pl.when(last)
        def _():
            finish(mine_total + up_in[k, z].astype(jnp.float32))

        @pl.when(jnp.logical_not(first | last))
        def _():
            finish(mine_total + up_in[k, z].astype(jnp.float32) + down_in[k, z].astype(jnp.float32))

        hand_on(k, z, z < m - 1, z > 0)
        for a, layer, row, rows, col, at in blocks(k):
            there, own = pl.ds(at, rows), own_slice(a, layer, row, rows, col)
            pltpu.make_async_copy(master.at[k, there], new_masters[a].at[own], total_sem.at[5]).start()
            pltpu.make_async_copy(moment.at[k, there], new_moments[a].at[own], total_sem.at[6]).start()

    def gather(g, k):
        low, high = z - g, z + g

        @pl.when(low >= 0)
        def _():
            wait_bytes(gathered.at[k, low], gather_sem.at[k, low])
            hand_on(k, low, z < m - 1, False)

        @pl.when(high < m)
        def _():
            wait_bytes(gathered.at[k, high], gather_sem.at[k, high])
            hand_on(k, high, False, z > 0)

    barrier = pltpu.get_barrier_semaphore()
    pl.semaphore_signal(barrier, inc=1, device_id={"rep": partner}, device_id_type=MESH)

    @pl.when(z > 0)
    def _():
        pl.semaphore_signal(barrier, inc=1, device_id={"rep": below}, device_id_type=MESH)

    @pl.when(z < m - 1)
    def _():
        pl.semaphore_signal(barrier, inc=1, device_id={"rep": above}, device_id_type=MESH)

    pl.semaphore_wait(barrier, 1 + (z > 0).astype(jnp.int32) + (z < m - 1).astype(jnp.int32))

    stages = [begin]
    stages += [functools.partial(forward, s) for s in range(1, m - 1)]
    stages += [update]
    stages += [functools.partial(gather, g) for g in range(1, m)]
    lead = min(LEAD, pieces)

    def early(k, carry):
        fetch(k)
        return carry

    lax.fori_loop(0, lead, early, 0)

    def tick(t, carry):
        @pl.when(t + lead < pieces)
        def _():
            fetch(t + lead)

        for s in reversed(range(len(stages))):
            k = t - s

            @pl.when((k >= 0) & (k < pieces))
            def _():
                stages[s](k)

        return carry

    lax.fori_loop(0, pieces + len(stages) - 1, tick, 0)

    wait_bytes(theirs, total_sem.at[0])
    wait_bytes(theirs.at[:, pl.ds(0, m - 1)], total_sem.at[1])
    for s in range(2, 5):
        wait_bytes(gathered, total_sem.at[s])
    wait_bytes(master, total_sem.at[5])
    wait_bytes(moment, total_sem.at[6])

    def drain(k, carry):
        for j in range(m):
            @pl.when((z < m - 1) & (j <= z))
            def _():
                wait_bytes(gathered.at[k, j], gather_up_sem.at[k, j])

            @pl.when((z > 0) & (j >= z))
            def _():
                wait_bytes(gathered.at[k, j], gather_down_sem.at[k, j])
        return carry

    lax.fori_loop(0, pieces, drain, 0)


def on_device(n, *arrays):
    states = arrays[1::3]
    own_shapes = [x.shape for x in states]
    pieces = PIECES
    while plan(own_shapes, pieces) is None:
        pieces //= 2
    cuts = plan(own_shapes, pieces)
    width = min(cols for _, _, _, cols in cuts)
    while any(cols % width for _, _, _, cols in cuts):
        width -= 128
    depth = sum(rows * (cols // width) for _, _, rows, cols in cuts)
    m = n // 2
    out_shape = []
    for delta, master, moment in zip(arrays[0::3], arrays[1::3], arrays[2::3]):
        out_shape += [
            jax.ShapeDtypeStruct(delta.shape[1:], jnp.bfloat16),
            jax.ShapeDtypeStruct(master.shape, jnp.float32),
            jax.ShapeDtypeStruct(moment.shape, jnp.float32),
        ]
    chunks = pltpu.VMEM((pieces, m, depth, width), jnp.bfloat16)
    state = pltpu.VMEM((pieces, depth, width), jnp.float32)
    flags = pltpu.SemaphoreType.DMA((pieces, m))
    return tuple(
        pl.pallas_call(
            functools.partial(kernel, n, cuts, width, own_shapes),
            out_shape=out_shape,
            in_specs=[pl.BlockSpec(memory_space=pl.ANY)] * len(arrays),
            out_specs=[pl.BlockSpec(memory_space=pl.ANY)] * len(out_shape),
            scratch_shapes=[chunks] * 5 + [state] * 2
            + [flags] * 5 + [pltpu.SemaphoreType.DMA((pieces,))] + [flags] * 2
            + [pltpu.SemaphoreType.DMA((7,))],
            compiler_params=pltpu.CompilerParams(
                collective_id=0, has_side_effects=True, vmem_limit_bytes=60 * 1024 * 1024
            ),
        )(*arrays)
    )


def solution(mesh):
    placed = (
        P("rep", None, None, "tp"),
        P(None, "rep", "tp"),
        P(None, "rep", "tp"),
        P("rep", None, None, "tp"),
        P(None, "rep", "tp"),
        P(None, "rep", "tp"),
        P("rep", None, "tp", None),
        P(None, "tp", "rep"),
        P(None, "tp", "rep"),
    )
    return jax.shard_map(
        functools.partial(on_device, mesh.shape["rep"]),
        mesh=mesh,
        in_specs=placed,
        out_specs=(
            P(None, None, "tp"),
            P(None, "rep", "tp"),
            P(None, "rep", "tp"),
            P(None, None, "tp"),
            P(None, "rep", "tp"),
            P(None, "rep", "tp"),
            P(None, "tp", None),
            P(None, "tp", "rep"),
            P(None, "tp", "rep"),
        ),
        check_vma=False,
    )
```

profile of v0, /device:TPU:0, one launch (start us, length us, event | category | flops | bytes accessed | tf_op | source)
XLA Modules:
  0.0 183.0 jit_solution(16027890545843431828)
XLA Ops:
  0.6 164.0 %shard_map.160 = (bf16[2,2048,768]{2,1,0:T(8,128)(2,1)}, f32[2,256,768]{2,1,0:T(8,128)}, f32[2,256,768]{2,1,0:T(8,128)}, bf16[2,512,1024]{2,1,0:T(8,128)(2,1)}, ...) custom-call(bf16[1,2,2048,768]{3,2,1,0:T(8,128)(2,1)} %refs_0_.1, ...), custom_call_target="tpu_custom_call" | custom-call | tf_op jit(solution)/shard_map/pallas_call | solution.py:295
  164.7 0.0 copy-start.3
  164.7 6.0 %copy.27 = bf16[2,2048,768]{2,1,0:T(8,128)(2,1)} copy(bf16[2,2048,768]{2,1,0:T(8,128)(2,1)} %get-tuple-element.18) | data formatting | bytes 12582912
  170.7 0.0 copy-done.3
  170.7 0.0 copy-start.2
  170.7 1.1 copy.28
  171.9 0.8 copy-done.2
  172.7 0.0 copy-start.1
  172.7 0.0 copy-start.7
  172.7 1.1 copy.29
  173.8 1.0 copy-done.1
  174.9 0.0 copy-start.6
  174.9 0.0 copy-start
  174.9 1.3 copy.30
  176.2 0.0 copy-done.7
  176.2 0.8 copy.31
  177.0 0.0 copy-done.6
  177.0 0.8 copy.32
  177.8 0.6 copy-done
  178.4 2.0 %copy.33 = bf16[2,512,2048]{2,1,0:T(8,128)(2,1)} copy(bf16[2,512,2048]{2,1,0:T(8,128)(2,1)S(1)} %copy-done) | data formatting | bytes 8388608
  180.4 0.0 copy-done.5
  180.4 1.0 copy.34
  181.4 0.6 copy-done.4
  182.0 1.0 copy.35
  (2 shorter events, 0.0 us)
Async XLA Ops:
  164.7 6.0 %copy-start.3 = (f32[2,256,768]{2,1,0:T(8,128)S(1)}, f32[2,256,768]{2,1,0:T(8,128)}, u32[]{:S(2)}) copy-start(f32[2,256,768]{2,1,0:T(8,128)} %get-tuple-element.19) | copy-start | bytes 4718596
  170.7 2.0 %copy-start.2 = (f32[2,256,768]{2,1,0:T(8,128)S(1)}, f32[2,256,768]{2,1,0:T(8,128)}, u32[]{:S(2)}) copy-start(f32[2,256,768]{2,1,0:T(8,128)} %get-tuple-element.20) | copy-start | bytes 4718596
  172.7 2.2 %copy-start.1 = (bf16[2,512,1024]{2,1,0:T(8,128)(2,1)S(1)}, bf16[2,512,1024]{2,1,0:T(8,128)(2,1)}, u32[]{:S(2)}) copy-start(bf16[2,512,1024]{2,1,0:T(8,128)(2,1)} %get-tuple-element.21) | copy-start | bytes 6291460
  172.7 3.5 %copy-start.7 = (f32[2,64,1024]{2,1,0:T(8,128)S(1)}, f32[2,64,1024]{2,1,0:T(8,128)}, u32[]{:S(2)}) copy-start(f32[2,64,1024]{2,1,0:T(8,128)} %get-tuple-element.22) | copy-start | bytes 1572868
  174.9 2.1 %copy-start.6 = (f32[2,64,1024]{2,1,0:T(8,128)S(1)}, f32[2,64,1024]{2,1,0:T(8,128)}, u32[]{:S(2)}) copy-start(f32[2,64,1024]{2,1,0:T(8,128)} %get-tuple-element.23) | copy-start | bytes 1572868
  174.9 3.5 %copy-start = (bf16[2,512,2048]{2,1,0:T(8,128)(2,1)S(1)}, bf16[2,512,2048]{2,1,0:T(8,128)(2,1)}, u32[]{:S(2)}) copy-start(bf16[2,512,2048]{2,1,0:T(8,128)(2,1)} %get-tuple-element.24) | copy-start | bytes 12582916
  178.4 2.0 %copy-start.5 = (f32[2,512,256]{2,1,0:T(8,128)S(1)}, f32[2,512,256]{2,1,0:T(8,128)}, u32[]{:S(2)}) copy-start(f32[2,512,256]{2,1,0:T(8,128)} %get-tuple-element.25) | copy-start | bytes 3145732
  180.4 1.6 copy-start.4
where the time goes:
time: 183 us
  Pallas kernels  164 us (90%)
  local copies, waits for them, and re-layouts  18.2 us (10%)
    pallas_call x1, Pallas kernels, on_device(): pl.pallas_call(functools.partial(kernel, n, cuts, width, own_shapes), out...  164 us
    unnamed x25, local copies, waits for them, and re-layouts  18.2 us

commit v1 on v0

v1 whole, which is shorter than its diff:
```python
import functools

import jax
import jax.numpy as jnp
from jax import lax
from jax.experimental import pallas as pl
from jax.experimental.pallas import tpu as pltpu
from jax.sharding import PartitionSpec as P

OUTER_RATE = 0.7
OUTER_MOMENTUM = 0.9
MESH = pl.DeviceIdType.MESH
PIECE_BYTES = 32 * 1024
SPACING = 6
LEAD = 8


class Piece:
    def __init__(self, whole, own, first):
        self.layers, self.own_rows, self.cols = own
        self.by_rows = whole[1] != own[1]
        self.rows = 16
        while (
            self.own_rows % (2 * self.rows) == 0
            and 4 * self.rows * self.cols <= PIECE_BYTES
        ):
            self.rows *= 2
        self.per_layer = self.own_rows // self.rows
        self.first = first
        self.count = self.layers * self.per_layer

    def own(self, layer, row):
        return (layer, pl.ds(pl.multiple_of(row, 16), self.rows))

    def whole(self, layer, row, owner):
        if self.by_rows:
            start = pl.multiple_of(owner * self.own_rows + row, 16)
            return (layer, pl.ds(start, self.rows))
        start = pl.multiple_of(owner * self.cols, 128)
        return (layer, pl.ds(pl.multiple_of(row, 16), self.rows), pl.ds(start, self.cols))


def exchange(n, cuts, *refs):
    deltas, masters, moments = refs[0:9:3], refs[1:9:3], refs[2:9:3]
    params, new_masters, new_moments = refs[9:18:3], refs[10:18:3], refs[11:18:3]
    theirs, mine, up_in, down_in = refs[18:21], refs[21:24], refs[24:27], refs[27:30]
    (theirs_sem, mine_sem, up_sem, down_sem, gather_sem,
     master_sem, moment_sem, total_sem) = refs[30:]
    m = n // 2
    phases = (m + 1) // 2
    pieces = sum(cut.count for cut in cuts)
    me = lax.axis_index("rep")
    z, core = me // 2, me % 2
    partner = z * 2 + 1 - core
    above, below = (z + 1) * 2 + core, (z - 1) * 2 + core
    first, last = z == 0, z == m - 1

    def remote(src, dst, send, recv, rank):
        return pltpu.make_async_remote_copy(
            src_ref=src, dst_ref=dst, send_sem=send, recv_sem=recv,
            device_id={"rep": rank}, device_id_type=MESH,
        )

    def wait_bytes(ref, sem):
        pltpu.make_async_copy(ref, ref, sem).wait()

    def visit(i, act):
        for a, cut in enumerate(cuts):
            @pl.when((i >= cut.first) & (i < cut.first + cut.count))
            def _():
                k = i - cut.first
                layer = lax.div(k, cut.per_layer)
                act(a, cut, layer, (k - layer * cut.per_layer) * cut.rows)

    def chunks_of(s):
        phase = sum((s >= q * pieces).astype(jnp.int32) for q in range(1, phases))
        return phase, m - 1 - phase, s - phase * pieces

    def fetch(s):
        low, high, i = chunks_of(s)

        def act(a, cut, layer, row):
            here = cut.own(layer, row)

            def chunk(j):
                remote(
                    deltas[a].at[(0,) + cut.whole(layer, row, 2 * j + 1 - core)],
                    theirs[a].at[(j,) + here], total_sem.at[0, a], theirs_sem.at[j, i], partner,
                ).start()
                pltpu.make_async_copy(
                    deltas[a].at[(0,) + cut.whole(layer, row, 2 * j + core)],
                    mine[a].at[(j,) + here], mine_sem.at[j, i],
                ).start()

            chunk(high)

            @pl.when(low != high)
            def _():
                chunk(low)

            @pl.when((z == low) | (z == high))
            def _():
                pltpu.make_async_copy(masters[a].at[here], new_masters[a].at[here], master_sem.at[i]).start()
                pltpu.make_async_copy(moments[a].at[here], new_moments[a].at[here], moment_sem.at[i]).start()

        visit(i, act)

    def pair_sum(a, at, i):
        wait_bytes(theirs[a].at[at], theirs_sem.at[at[0], i])
        wait_bytes(mine[a].at[at], mine_sem.at[at[0], i])
        return theirs[a][at].astype(jnp.float32) + mine[a][at].astype(jnp.float32)

    def reduce(s, up):
        low, high, i = chunks_of(s)
        arrived, sem, target, starts = (up_in, up_sem, above, first) if up else (down_in, down_sem, below, last)

        def act(a, cut, layer, row):
            for j, other in ((high, low), (low, high)) if up else ((low, high), (high, low)):
                wanted = (j > z) if up else (j < z)
                if j is (low if up else high):
                    wanted = wanted & (j != other)
                at = (j,) + cut.own(layer, row)

                @pl.when(wanted & starts)
                def _():
                    mine[a][at] = pair_sum(a, at, i).astype(jnp.bfloat16)

                @pl.when(wanted & jnp.logical_not(starts))
                def _():
                    total = pair_sum(a, at, i)
                    wait_bytes(arrived[a].at[at], sem.at[j, i])
                    mine[a][at] = (total + arrived[a][at].astype(jnp.float32)).astype(jnp.bfloat16)

                @pl.when(wanted)
                def _():
                    remote(mine[a].at[at], arrived[a].at[at], total_sem.at[1, a], sem.at[j, i], target).start()

        visit(i, act)

    def hand_on(a, cut, layer, row, j, i, up, down):
        there = params[a].at[cut.whole(layer, row, 2 * j + core)]

        @pl.when(up)
        def _():
            remote(there, there, total_sem.at[4, a], gather_sem.at[j, i], above).start()

        @pl.when(down)
        def _():
            remote(there, there, total_sem.at[4, a], gather_sem.at[j, i], below).start()

        remote(there, there, total_sem.at[2, a], total_sem.at[3, a], partner).start()

    def update(i):
        def act(a, cut, layer, row):
            here = cut.own(layer, row)
            at = (z,) + here
            total = pair_sum(a, at, i)
            wait_bytes(new_masters[a].at[here], master_sem.at[i])
            wait_bytes(new_moments[a].at[here], moment_sem.at[i])

            @pl.when(z > 0)
            def _():
                wait_bytes(up_in[a].at[at], up_sem.at[z, i])

            @pl.when(z < m - 1)
            def _():
                wait_bytes(down_in[a].at[at], down_sem.at[z, i])

            def finish(summed):
                average = summed / n
                momentum = OUTER_MOMENTUM * new_moments[a][here] + average
                updated = new_masters[a][here] - OUTER_RATE * (average + OUTER_MOMENTUM * momentum)
                new_moments[a][here] = momentum
                new_masters[a][here] = updated
                params[a][cut.whole(layer, row, me)] = updated.astype(jnp.bfloat16)

            @pl.when(first)
            def _():
                finish(total + down_in[a][at].astype(jnp.float32))

            @pl.when(last)
            def _():
                finish(total + up_in[a][at].astype(jnp.float32))

            @pl.when(jnp.logical_not(first | last))
            def _():
                finish(total + up_in[a][at].astype(jnp.float32) + down_in[a][at].astype(jnp.float32))

            hand_on(a, cut, layer, row, z, i, z < m - 1, z > 0)

        visit(i, act)

    def gather(j, i):
        def act(a, cut, layer, row):
            wait_bytes(params[a].at[cut.whole(layer, row, 2 * j + core)], gather_sem.at[j, i])
            hand_on(a, cut, layer, row, j, i, (j < z) & (z < m - 1), (j > z) & (z > 0))

        visit(i, act)

    barrier = pltpu.get_barrier_semaphore()
    pl.semaphore_signal(barrier, inc=1, device_id={"rep": partner}, device_id_type=MESH)

    @pl.when(z > 0)
    def _():
        pl.semaphore_signal(barrier, inc=1, device_id={"rep": below}, device_id_type=MESH)

    @pl.when(z < m - 1)
    def _():
        pl.semaphore_signal(barrier, inc=1, device_id={"rep": above}, device_id_type=MESH)

    pl.semaphore_wait(barrier, 1 + (z > 0).astype(jnp.int32) + (z < m - 1).astype(jnp.int32))

    steps = phases * pieces
    lead = min(LEAD, steps)

    def early(s, carry):
        fetch(s)
        return carry

    lax.fori_loop(0, lead, early, 0)

    def tick(t, carry):
        @pl.when(t + lead < steps)
        def _():
            fetch(t + lead)

        for j in range(m):
            near = min(j, m - 1 - j)
            distance = jnp.where(z > j, z - j, j - z)
            i = t - near * pieces - SPACING * (m - 1 - near + distance)

            @pl.when((z != j) & (i >= 0) & (i < pieces))
            def _():
                gather(j, i)

        near = jnp.minimum(z, m - 1 - z)
        i = t - near * pieces - SPACING * (m - 1 - near)

        @pl.when((i >= 0) & (i < pieces))
        def _():
            update(i)

        up = t - SPACING * z

        @pl.when((z < m - 1) & (up >= 0) & (up < steps))
        def _():
            reduce(up, True)

        down = t - SPACING * (m - 1 - z)

        @pl.when((z > 0) & (down >= 0) & (down < steps))
        def _():
            reduce(down, False)

        return carry

    longest = max(
        near * pieces + SPACING * (m - 1 - near + max(j, m - 1 - j))
        for j in range(m)
        for near in [min(j, m - 1 - j)]
    )
    lax.fori_loop(0, longest + pieces, tick, 0)

    for a in range(len(cuts)):
        passed = theirs[a].at[pl.ds(0, m - 1)]
        wait_bytes(theirs[a], total_sem.at[0, a])
        wait_bytes(passed, total_sem.at[1, a])
        wait_bytes(theirs[a], total_sem.at[2, a])
        wait_bytes(theirs[a], total_sem.at[3, a])
        wait_bytes(theirs[a].at[0], total_sem.at[4, a])

        @pl.when(jnp.logical_not(first | last))
        def _():
            wait_bytes(theirs[a], total_sem.at[4, a])


def store(parts, *refs):
    count = len(refs) // 2
    held, out, sem = refs[:count], refs[count:2 * count], refs[2 * count]
    for a in range(count):
        for layer in range(held[a].shape[0]):
            pltpu.make_async_copy(held[a].at[layer], out[a].at[layer], sem.at[a]).start()
    for a in range(count):
        pltpu.make_async_copy(held[a], out[a], sem.at[a]).wait()


def on_device(n, *arrays):
    cuts, first = [], 0
    for delta, master in zip(arrays[0::3], arrays[1::3]):
        cut = Piece(delta.shape[1:], master.shape, first)
        cuts.append(cut)
        first += cut.count
    m = n // 2
    held, out_shape = [], []
    for delta, master in zip(arrays[0::3], arrays[1::3]):
        for shape, dtype in (
            (delta.shape[1:], jnp.bfloat16),
            (master.shape, jnp.float32),
            (master.shape, jnp.float32),
        ):
            held.append(pltpu.VMEM(shape, dtype))
            out_shape.append(jax.ShapeDtypeStruct(shape, dtype))
    anywhere = pl.BlockSpec(memory_space=pl.ANY)
    chunks = [pltpu.VMEM((m, *master.shape), jnp.bfloat16) for master in arrays[1::3]]
    flags = pltpu.SemaphoreType.DMA((m, first))
    results = pl.pallas_call(
        functools.partial(exchange, n, cuts),
        out_shape=held,
        in_specs=[anywhere] * len(arrays),
        out_specs=[pl.BlockSpec(memory_space=pltpu.VMEM)] * len(held),
        scratch_shapes=chunks * 4 + [flags] * 5
        + [pltpu.SemaphoreType.DMA((first,))] * 2 + [pltpu.SemaphoreType.DMA((5, len(cuts)))],
        compiler_params=pltpu.CompilerParams(
            collective_id=0, has_side_effects=True, vmem_limit_bytes=44 * 1024 * 1024
        ),
    )(*arrays)
    return tuple(
        pl.pallas_call(
            functools.partial(store, 1),
            out_shape=out_shape,
            in_specs=[anywhere] * len(out_shape),
            out_specs=[anywhere] * len(out_shape),
            scratch_shapes=[pltpu.SemaphoreType.DMA((len(out_shape),))],
            compiler_params=pltpu.CompilerParams(vmem_limit_bytes=1024 * 1024),
        )(*results)
    )


def solution(mesh):
    placed = (
        P("rep", None, None, "tp"),
        P(None, "rep", "tp"),
        P(None, "rep", "tp"),
        P("rep", None, None, "tp"),
        P(None, "rep", "tp"),
        P(None, "rep", "tp"),
        P("rep", None, "tp", None),
        P(None, "tp", "rep"),
        P(None, "tp", "rep"),
    )
    return jax.shard_map(
        functools.partial(on_device, mesh.shape["rep"]),
        mesh=mesh,
        in_specs=placed,
        out_specs=(
            P(None, None, "tp"),
            P(None, "rep", "tp"),
            P(None, "rep", "tp"),
            P(None, None, "tp"),
            P(None, "rep", "tp"),
            P(None, "rep", "tp"),
            P(None, "tp", None),
            P(None, "tp", "rep"),
            P(None, "tp", "rep"),
        ),
        check_vma=False,
    )
```

time: 183 us -> 177 us (0.967)
  local copies, waits for them, and re-layouts: 18.2 us -> 0 us
  Pallas kernels: 164 us -> 176 us
    unnamed x25 -> x0, local copies, waits for them, and re-layouts: 18.2 us -> none
    pallas_call x1 -> x2, Pallas kernels: 164 us -> 176 us  [the longest x1 170 us: on_device(): pl.pallas_call(functools.partial(exchange, n, cuts), out_shape=held, in_s...]
where the time goes in v1:
time: 177 us
  Pallas kernels  176 us (99%)
    pallas_call x1, Pallas kernels, on_device(): pl.pallas_call(functools.partial(exchange, n, cuts), out_shape=held, in_s...  170 us
    pallas_call x1, Pallas kernels, on_device(): pl.pallas_call(functools.partial(store, 1), out_shape=out_shape, in_specs...  6.58 us

profile of v1, /device:TPU:0, one launch (start us, length us, event | category | flops | bytes accessed | tf_op | source)
XLA Modules:
  0.0 176.9 jit_solution(7240610511206182082)
XLA Ops:
  0.6 169.7 %shard_map.160 = (bf16[2,2048,768]{2,1,0:T(8,128)(2,1)S(1)}, f32[2,256,768]{2,1,0:T(8,128)S(1)}, f32[2,256,768]{2,1,0:T(8,128)S(1)}, bf16[2,512,1024]{2,1,0:T(8,...) custom-call(bf16[1,2,2048,768]{3,2,1,0:T(8,128)(2,1)} %refs_0_.1, ...), custom_call_target="tpu_custom_call" | custom-call | tf_op jit(solution)/shard_map/pallas_call | solution.py:306
  170.3 6.6 %shard_map.161 = (bf16[2,2048,768]{2,1,0:T(8,128)(2,1)}, f32[2,256,768]{2,1,0:T(8,128)}, f32[2,256,768]{2,1,0:T(8,128)}, bf16[2,512,1024]{2,1,0:T(8,128)(2,1)}, ...) custom-call(bf16[2,2048,768]{2,1,0:T(8,128)(2,1)S(1)} %get-tuple-ele, ...), custom_call_target="tpu_custom_call" | custom-call | tf_op jit(solution)/shard_map/pallas_call | solution.py:318
